TPU v7x, 8 devices: a whole 2x2x1 slice. The times are simulated.
8 devices in a mesh: dp: 1 (over z), col: 2 (over y), row: 4 (over x, core).
Axes of the slice: x: 2, y: 2, z: 1, core: 2. Of those that a mesh axis runs over, the one named last changes fastest.
Arguments:
- x_in: bfloat16 [2, 4096, 1024], P(None, ('dp', 'row'), 'col')
- ln_gamma: float32 [1024], P('col')
- w_in: bfloat16 [1024, 4096], P('row', 'col')
- w_out: bfloat16 [4096, 1024], P('row', 'col')
Outputs:
- output: bfloat16 [2, 4096, 1024], P(None, ('dp', 'row'), 'col')
All inputs are finite; a program needn't handle non-finite values.
Results may differ from a plain program's by a relative error of at most 0.001.
Values are sent between devices in bfloat16 or wider.
A program may use at most 1 GiB of HBM per device.

v0:
```python
import jax
import jax.numpy as jnp
from jax import lax
from jax.sharding import PartitionSpec as P

LN_EPS = 1e-5


def solution(mesh):
    col_size = mesh.shape["col"]
    act_spec = P(None, ("dp", "row"), "col")

    def per_device(x_blk, gamma_blk, w_in_blk, w_out_blk):
        d_model = gamma_blk.shape[0] * col_size
        x_f32 = x_blk.astype(jnp.float32)
        row_stats = jnp.stack([jnp.sum(x_f32, axis=-1), jnp.sum(x_f32 * x_f32, axis=-1)])
        row_stats = lax.psum(row_stats, "col")
        row_mean = row_stats[0] / d_model
        row_var = row_stats[1] / d_model - row_mean * row_mean
        inv_std = lax.rsqrt(row_var + LN_EPS)
        z_norm = ((x_f32 - row_mean[..., None]) * inv_std[..., None] * gamma_blk).astype(jnp.bfloat16)
        z_panel = lax.all_gather(z_norm, "col", axis=2, tiled=True)
        w_in_panel = lax.all_gather(w_in_blk, "row", axis=0, tiled=True)
        hidden = jnp.dot(z_panel, w_in_panel, preferred_element_type=jnp.float32)
        hidden = jax.nn.gelu(hidden, approximate=True).astype(jnp.bfloat16)
        h_panel = lax.all_gather(hidden, "col", axis=2, tiled=True)
        w_out_panel = lax.all_gather(w_out_blk, "row", axis=0, tiled=True)
        branch = jnp.dot(h_panel, w_out_panel, preferred_element_type=jnp.float32)
        return (x_f32 + branch).astype(jnp.bfloat16)

    return jax.shard_map(per_device, mesh=mesh, in_specs=(act_spec, P("col"), P("row", "col"), P("row", "col")), out_specs=act_spec, check_vma=False)
```

profile of v0, /device:TPU:0, one launch (start us, length us, event | category | flops | bytes accessed | tf_op | source)
XLA Modules:
  0.0 361.6 jit_solution(17899703283188205468)
XLA Ops:
  6.5 0.0 all-gather.5.cloned.1.call-start
  6.5 2.3 convert_reduce_fusion
  8.8 10.1 %psum.7 = f32[2,2,1024]{2,1,0:T(2,128)S(1)} all-reduce(f32[2,2,1024]{2,1,0:T(2,128)S(1)} %pad_maximum_fusion), channel_id=1, replica_groups=mesh['dp'=1,'col'=2,'row'=4] {'col'}, use_global_device_ids=true, to_apply=%region_2.0 | all-reduce | flops 4096 | bytes 32768 | tf_op jit(solution)/shard_map/psum | solution.py:17
  18.9 3.1 fusion.11
  22.0 0.0 all-gather.5.cloned.1.call-update
  22.0 0.0 all-gather.7.cloned.1.call-start
  22.1 0.7 all-gather.7.cloned.1.call-update
  22.8 0.0 all-gather.11.cloned.1.call-start
  22.8 0.7 all-gather.11.cloned.1.call-update
  23.5 0.0 all-gather.9.cloned.1.call-start
  23.6 52.8 %all-gather.5.cloned.1.call-done = bf16[2,1024,1024]{2,1,0:T(8,128)(2,1)} async-done(((bf16[2,1024,512]{2,1,0:T(8,128)(2,1)}), bf16[2,1024,1024]{2,1,0:T(8,128)(2,1)}) %all-gather.5.cloned.1.call-update) | async-done | bytes 4194320 | tf_op jit(solution)/shard_map/all_gather | solution.py:22
  76.3 33.1 %all-gather.7.cloned.1.call-done = bf16[1024,2048]{1,0:T(8,128)(2,1)} async-done(((bf16[256,2048]{1,0:T(8,128)(2,1)}), bf16[1024,2048]{1,0:T(8,128)(2,1)}) %all-gather.7.cloned.1.call-update) | async-done | bytes 4194320 | tf_op jit(solution)/shard_map/all_gather | solution.py:23
  109.4 17.4 %fusion.7 = bf16[2,1024,2048]{2,1,0:T(8,128)(2,1)} fusion(bf16[2,1024,1024]{2,1,0:T(8,128)(2,1)} %all-gather.5.cloned.1.call-done, bf16[1024,2048]{1,0:T(8,128)(2,1)} %all-gather.7.cloned.1.call-done), kind=kOutput, calls=%fused_computation.8 | convolution fusion | flops 8627683328 | bytes 16777216 | tf_op jit(solution)/shard_map/dot_general | solution.py:24
  126.8 0.0 copy-start
  126.8 0.0 all-gather.9.cloned.1.call-update
  126.8 15.6 %all-gather.11.cloned.1.call-done = bf16[4096,512]{1,0:T(8,128)(2,1)} async-done(((bf16[1024,512]{1,0:T(8,128)(2,1)}), bf16[4096,512]{1,0:T(8,128)(2,1)}) %all-gather.11.cloned.1.call-update) | async-done | bytes 4194320 | tf_op jit(solution)/shard_map/all_gather | solution.py:27
  142.5 198.1 %all-gather.9.cloned.1.call-done = bf16[2,1024,4096]{2,1,0:T(8,128)(2,1)} async-done(((bf16[2,1024,2048]{2,1,0:T(8,128)(2,1)}), bf16[2,1024,4096]{2,1,0:T(8,128)(2,1)}) %all-gather.9.cloned.1.call-update) | async-done | bytes 16777232 | tf_op jit(solution)/shard_map/all_gather | solution.py:26
  340.6 0.0 copy-done
  340.6 14.5 %fusion.12 = bf16[2,1024,512]{2,1,0:T(8,128)(2,1)} fusion(bf16[2,1024,512]{2,1,0:T(8,128)(2,1)S(1)} %copy-done, bf16[2,1024,4096]{2,1,0:T(8,128)(2,1)} %all-gather.9.cloned.1.call-done, bf16[4096,512]{1,0:T(8,128)(2,1)} %all-gather.11.cloned.1.call-done), kind=kOutput, calls=%fused_computation.17 | convolution fusion | flops 8593080320 | bytes 25165824 | tf_op jit(solution)/shard_map/dot_general | solution.py:28
  (3 shorter events, 0.0 us)
Async XLA Ops:
  6.5 69.8 %all-gather.5.cloned.1.call-start = ((), (), s32[]{:S(2)}) async-start(), calls=%async_computation | async-start | bytes 6291456 | tf_op jit(solution)/shard_map/all_gather | solution.py:22
  22.0 87.4 %all-gather.7.cloned.1.call-start = ((), (), s32[]{:S(2)}) async-start(), calls=%async_computation.1 | async-start | bytes 5242880 | tf_op jit(solution)/shard_map/all_gather | solution.py:23
  22.8 119.7 %all-gather.11.cloned.1.call-start = ((), (), s32[]{:S(2)}) async-start(), calls=%async_computation.3 | async-start | bytes 5242880 | tf_op jit(solution)/shard_map/all_gather | solution.py:27
  23.5 317.0 %all-gather.9.cloned.1.call-start = ((), (), s32[]{:S(2)}) async-start(), calls=%async_computation.2 | async-start | bytes 25165824 | tf_op jit(solution)/shard_map/all_gather | solution.py:26
  126.8 213.8 %copy-start = (bf16[2,1024,512]{2,1,0:T(8,128)(2,1)S(1)}, bf16[2,1024,512]{2,1,0:T(8,128)(2,1)}, u32[]{:S(2)}) copy-start(bf16[2,1024,512]{2,1,0:T(8,128)(2,1)} %param.4) | copy-start | bytes 6291460
Sparse Core Ops, SparseCore 0:
  22.1 54.1 all-gather.4
  77.9 31.4 all-gather.6
  110.9 31.4 all-gather.10
  143.8 196.6 all-gather.8
where the time goes:
time: 362 us
  waiting for transfers between devices  301 us (83%)
  matrix products  31.9 us (9%)
  between operations  13.1 us (4%)
  blocking collectives  10.1 us (3%)
  other arithmetic  5.36 us (1%)
    all_gather x1, waiting for transfers between devices, per_device(): h_panel = lax.all_gather(hidden, 'col', axis=2, tiled=True)  198 us
    all_gather x1, waiting for transfers between devices, per_device(): z_panel = lax.all_gather(z_norm, 'col', axis=2, tiled=True)  52.8 us
    all_gather x1, waiting for transfers between devices, per_device(): w_in_panel = lax.all_gather(w_in_blk, 'row', axis=0, tiled=True)  33.1 us
    dot_general x1, matrix products, per_device(): hidden = jnp.dot(z_panel, w_in_panel, preferred_element_type=jnp.float32)  17.4 us
    all_gather x1, waiting for transfers between devices, per_device(): w_out_panel = lax.all_gather(w_out_blk, 'row', axis=0, tiled=True)  15.6 us
    dot_general x1, matrix products, per_device(): branch = jnp.dot(h_panel, w_out_panel, preferred_element_type=jnp.float32)  14.5 us
    psum x1, blocking collectives, per_device(): row_stats = lax.psum(row_stats, 'col')  10.1 us
  transfers between devices with their start and end apart: 4, of which 4 were waited for; matrix products, arithmetic and copies ran while one was open for 5% of the time, Pallas kernels for 0%

commit v1 on v0

v1 whole, which is shorter than its diff:
```python
import functools

import jax
import jax.numpy as jnp
from jax import lax
from jax.experimental import pallas as pl
from jax.experimental.pallas import tpu as pltpu
from jax.sharding import PartitionSpec as P

LN_EPS = 1e-5
MESH = pl.DeviceIdType.MESH
TC = 256
PC = 256
SQRT_2_OVER_PI = 0.7978845608028654

KINDS = dict(w1x=8, w1y=8, w1d=8, w1xd=8, w1yx=8, w1yd=8, w1dd=8, w2x=4, w2d=4, w2xd=4, x=8, g=1)
BASE = {}
_n = 0
for _k, _c in KINDS.items():
    BASE[_k] = _n
    _n += _c
N_COPIES = _n


def gelu(u):
    inner = u * (SQRT_2_OVER_PI + (SQRT_2_OVER_PI * 0.044715) * (u * u))
    return ((0.5 * u) * (1.0 + jnp.tanh(inner))).astype(jnp.bfloat16)


def kernel(x_hbm, g_hbm, w1_hbm, w2_hbm, y_hbm, xs, gs, w1s, w2s, zs, acc, ys, load_sem, out_sem, send_sem, recv_sem):
    n_chunks = xs.shape[1]
    n_w2 = w2_hbm.shape[0] // PC
    rows1 = w1_hbm.shape[0]
    d_model = zs.shape[2]
    half_d = d_model // 2

    col = lax.axis_index("col")
    row = lax.axis_index("row")
    row_p = row + 1 - 2 * (row % 2)
    row_x = (row + 2) % 4
    row_xp = (row_p + 2) % 4
    other = 1 - col
    partner, x_nbr, y_nbr = {"row": row_p}, {"row": row_x}, {"col": other}

    def piece(half, e):
        return half * 8 + (e % 2) * 4 + e // 2

    def blk(half, e, r):
        return w1s.at[piece(half, e), pl.ds(pl.multiple_of(r * rows1, rows1), rows1)]

    def w2p(r, j):
        return w2s.at[r * n_w2 + j]

    table = dict(
        w1x=(x_nbr, lambda e: blk(col, e, row), lambda e: blk(col, e, row_x)),
        w1y=(y_nbr, lambda e: blk(col, e, row), lambda e: blk(other, e, row)),
        w1d=(partner, lambda e: blk(col, e, row), lambda e: blk(col, e, row_p)),
        w1xd=(partner, lambda e: blk(col, e, row_x), lambda e: blk(col, e, row_xp)),
        w1yx=(x_nbr, lambda e: blk(other, e, row), lambda e: blk(other, e, row_x)),
        w1yd=(partner, lambda e: blk(other, e, row), lambda e: blk(other, e, row_p)),
        w1dd=(partner, lambda e: blk(other, e, row_x), lambda e: blk(other, e, row_xp)),
        w2x=(x_nbr, lambda j: w2p(row, j), lambda j: w2p(row_x, j)),
        w2d=(partner, lambda j: w2p(row, j), lambda j: w2p(row_p, j)),
        w2xd=(partner, lambda j: w2p(row_x, j), lambda j: w2p(row_xp, j)),
        x=(y_nbr, lambda i: xs.at[col, i], lambda i: xs.at[other, i]),
        g=(y_nbr, lambda i: gs.at[col], lambda i: gs.at[other]),
    )

    def copy(kind, i, ref):
        k = BASE[kind] + i
        return pltpu.make_async_remote_copy(
            src_ref=ref, dst_ref=ref, send_sem=send_sem.at[k], recv_sem=recv_sem.at[k],
            device_id=table[kind][0], device_id_type=MESH)

    def send(kind, i):
        copy(kind, i, table[kind][1](i)).start()

    def arrive(kind, i):
        copy(kind, i, table[kind][2](i)).wait_recv()

    loads = {}

    def load(key, src, dst):
        loads[key] = pltpu.make_async_copy(src, dst, load_sem.at[len(loads)])
        loads[key].start()

    def load_w1(e):
        cols = pl.ds(pl.multiple_of((e % 2) * (4 * PC) + (e // 2) * PC, PC), PC)
        load(("w1", e), w1_hbm.at[:, cols], blk(col, e, row))

    load("g", g_hbm, gs.at[col])
    for s in range(4):
        load_w1(2 * s)
        load_w1(2 * s + 1)
        load(("w2", s), w2_hbm.at[pl.ds(s * PC, PC)], w2p(row, s))
        for i in (2 * s, 2 * s + 1):
            load(("x", i), x_hbm.at[i], xs.at[col, i])

    barrier = pltpu.get_barrier_semaphore()
    for dev in (partner, x_nbr, y_nbr):
        pl.semaphore_signal(barrier, inc=1, device_id=dev, device_id_type=MESH)
    pl.semaphore_wait(barrier, 3)

    loads["g"].wait()
    send("g", 0)

    def issue(s):
        for e in (2 * s, 2 * s + 1):
            loads[("w1", e)].wait()
            send("w1x", e)
            send("w1d", e)
        loads[("w2", s)].wait()
        send("w2x", s)
        send("w2d", s)
        for i in (2 * s, 2 * s + 1):
            loads[("x", i)].wait()
            send("x", i)

    def layer_norm(i):
        rb = 64

        def step(t, _):
            rows = pl.ds(pl.multiple_of(t * rb, rb), rb)
            parts = [xs[h, i, rows, :].astype(jnp.float32) for h in range(2)]
            mean = sum(jnp.sum(v, axis=-1, keepdims=True) for v in parts) / d_model
            var = sum(jnp.sum(v * v, axis=-1, keepdims=True) for v in parts) / d_model - mean * mean
            inv = lax.rsqrt(var + LN_EPS)
            for h in range(2):
                zs[i, rows, h * half_d:(h + 1) * half_d] = ((parts[h] - mean) * inv * gs[h]).astype(jnp.bfloat16)
            acc[i, rows, :] = xs[col, i, rows, :].astype(jnp.float32)
            return 0

        lax.fori_loop(0, TC // rb, step, 0)

    def tile(c, pieces):
        z = zs[c]
        out = None
        for p in pieces:
            h = gelu(jnp.dot(z, w1s[p], preferred_element_type=jnp.float32))
            term = jnp.dot(h, w2s[p], preferred_element_type=jnp.float32)
            out = term if out is None else out + term
        acc[c] += out

    def pair(half, j):
        return piece(half, 2 * j), piece(half, 2 * j + 1)

    def run(lo, hi, f):
        lax.fori_loop(lo, hi, lambda t, _: (f(t), 0)[1], 0)

    issue(0)
    issue(1)
    arrive("g", 0)
    for s in range(4):
        if s + 2 < 4:
            issue(s + 2)
        if s == 2:
            for e in range(8):
                send("w1y", e)
        for e in (2 * s, 2 * s + 1):
            arrive("w1x", e)
            send("w1xd", e)
        arrive("w2x", s)
        send("w2xd", s)
        for i in (2 * s, 2 * s + 1):
            arrive("x", i)
            layer_norm(i)
        for e in (2 * s, 2 * s + 1):
            arrive("w1d", e)
            arrive("w1xd", e)
        arrive("w2d", s)
        arrive("w2xd", s)
        run(0, 2 * s + 2, lambda c: tile(c, pair(col, s)))
        if s > 0:
            run(0, 2 * s, lambda t: tile(2 * s + t % 2, pair(col, t // 2)))

    def forward(e):
        arrive("w1y", e)
        send("w1yx", e)
        send("w1yd", e)

    forward(0)
    forward(1)
    for e in range(8):
        if e + 2 < 8:
            forward(e + 2)
        arrive("w1yx", e)
        send("w1dd", e)
        arrive("w1yd", e)
        arrive("w1dd", e)
        p = piece(other, e)
        if e < 7:
            run(0, n_chunks, lambda c: tile(c, (p,)))
        else:
            def last(c):
                tile(c, (p,))
                ys[c] = acc[c].astype(jnp.bfloat16)
                pltpu.make_async_copy(ys.at[c], y_hbm.at[c], out_sem.at[c]).start()

            run(0, n_chunks, last)

    for kind, count in KINDS.items():
        for i in range(count):
            copy(kind, i, table[kind][1](i)).wait_send()
    for c in range(n_chunks):
        pltpu.make_async_copy(ys.at[c], y_hbm.at[c], out_sem.at[c]).wait()


def solution(mesh):
    act_spec = P(None, ("dp", "row"), "col")

    def per_device(x_blk, gamma_blk, w_in_blk, w_out_blk):
        batch, tokens, feats = x_blk.shape
        rows1, cols1 = w_in_blk.shape
        n_chunks = batch * tokens // TC
        d_model = 2 * feats
        n_pieces = 2 * cols1 // PC
        n_loads = 1 + cols1 // PC + w_out_blk.shape[0] // PC + n_chunks
        y = pl.pallas_call(
            kernel,
            name="mlp",
            out_shape=jax.ShapeDtypeStruct((n_chunks, TC, feats), jnp.bfloat16),
            in_specs=[pl.BlockSpec(memory_space=pl.ANY)] * 4,
            out_specs=pl.BlockSpec(memory_space=pl.ANY),
            scratch_shapes=[
                pltpu.VMEM((2, n_chunks, TC, feats), jnp.bfloat16),
                pltpu.VMEM((2, 1, feats), jnp.float32),
                pltpu.VMEM((n_pieces, d_model, PC), jnp.bfloat16),
                pltpu.VMEM((n_pieces, PC, feats), jnp.bfloat16),
                pltpu.VMEM((n_chunks, TC, d_model), jnp.bfloat16),
                pltpu.VMEM((n_chunks, TC, feats), jnp.float32),
                pltpu.VMEM((n_chunks, TC, feats), jnp.bfloat16),
                pltpu.SemaphoreType.DMA((n_loads,)),
                pltpu.SemaphoreType.DMA((n_chunks,)),
                pltpu.SemaphoreType.DMA((N_COPIES,)),
                pltpu.SemaphoreType.DMA((N_COPIES,)),
            ],
            compiler_params=pltpu.CompilerParams(collective_id=0, has_side_effects=True, vmem_limit_bytes=48 * 1024 * 1024),
        )(x_blk.reshape(n_chunks, TC, feats), gamma_blk.reshape(1, feats), w_in_blk, w_out_blk)
        return y.reshape(x_blk.shape)

    return jax.shard_map(per_device, mesh=mesh, in_specs=(act_spec, P("col"), P("row", "col"), P("row", "col")), out_specs=act_spec, check_vma=False)
```

time: 362 us -> 120 us (0.33)
  waiting for transfers between devices: 301 us -> 0 us
  Pallas kernels: 0 us -> 116 us
  matrix products: 31.9 us -> 0 us
  between operations: 13.1 us -> 0.01 us
  blocking collectives: 10.1 us -> 0 us
  other arithmetic: 5.36 us -> 0 us
  local copies, waits for them, and re-layouts: 0.01 us -> 4.45 us
    all_gather x4 -> x0, waiting for transfers between devices: 300 us -> none  [the longest x1 198 us: per_device(): h_panel = lax.all_gather(hidden, 'col', axis=2, tiled=True)]
    pallas_call x0 -> x1, Pallas kernels: none -> 116 us  [per_device(): pl.pallas_call(kernel, name='mlp', out_shape=jax.ShapeDtypeStruct((n_chun...]
    dot_general x2 -> x0, matrix products: 31.9 us -> none  [the longest x1 17.4 us: per_device(): hidden = jnp.dot(z_panel, w_in_panel, preferred_element_type=jnp.float32)]
    psum x1 -> x0, blocking collectives: 10.1 us -> none  [per_device(): row_stats = lax.psum(row_stats, 'col')]
    unnamed x2 -> x7, local copies, waits for them, and re-layouts: 0.01 us -> 4.45 us
  transfers between devices with their start and end apart: 4 -> 0, of which waited for: 4 -> 0; matrix products, arithmetic and copies ran while one was open for 5% -> 0% of each run, Pallas kernels for 0% -> 0%
where the time goes in v1:
time: 120 us
  Pallas kernels  116 us (97%)
  local copies, waits for them, and re-layouts  4.45 us (4%)
    pallas_call x1, Pallas kernels, per_device(): pl.pallas_call(kernel, name='mlp', out_shape=jax.ShapeDtypeStruct((n_chun...  116 us
    unnamed x7, local copies, waits for them, and re-layouts  4.45 us

profile of v1, /device:TPU:0, one launch (start us, length us, event | category | flops | bytes accessed | tf_op | source)
XLA Modules:
  0.0 120.2 jit_solution(2578658598359351263)
XLA Ops:
  0.0 0.0 copy-start
  0.0 1.2 %copy-done = bf16[256,2048]{1,0:T(8,128)(2,1)S(1)} copy-done((bf16[256,2048]{1,0:T(8,128)(2,1)S(1)}, bf16[256,2048]{1,0:T(8,128)(2,1)}, u32[]{:S(2)}) %copy-start) | copy-done | bytes 1048600
  1.2 0.0 copy-start.1
  1.2 1.2 %copy-done.1 = bf16[1024,512]{1,0:T(8,128)(2,1)S(1)} copy-done((bf16[1024,512]{1,0:T(8,128)(2,1)S(1)}, bf16[1024,512]{1,0:T(8,128)(2,1)}, u32[]{:S(2)}) %copy-start.1) | copy-done | bytes 1048600
  2.5 0.0 copy-start.2
  2.5 0.7 copy-done.2
  3.1 115.7 %mlp.1 = bf16[8,256,512]{2,1,0:T(8,128)(2,1)S(1)} custom-call(bf16[8,256,512]{2,1,0:T(8,128)(2,1)} %bitcast.5, f32[1,512]{1,0:T(1,128)S(1)} %bitcast.4, bf16[256,2048]{1,0:T(8,128)(2,1)S(1)} %copy-done, bf16[1024,512]{1,0:T(8,128)(2,1)S(1)} %copy-done.1), custom_call_target="tpu_custom_call" | custom-call | tf_op jit(solution)/shard_map/mlp/pallas_call | solution.py:218
  118.9 1.3 %copy.6 = bf16[2,1024,512]{2,1,0:T(8,128)(2,1)} copy(bf16[2,1024,512]{2,1,0:T(8,128)(2,1)S(1)} %bitcast.3) | data formatting | bytes 4194304
Async XLA Ops:
  0.0 1.2 %copy-start = (bf16[256,2048]{1,0:T(8,128)(2,1)S(1)}, bf16[256,2048]{1,0:T(8,128)(2,1)}, u32[]{:S(2)}) copy-start(bf16[256,2048]{1,0:T(8,128)(2,1)} %w1_hbm.1) | copy-start | bytes 3145732
  1.2 1.2 %copy-start.1 = (bf16[1024,512]{1,0:T(8,128)(2,1)S(1)}, bf16[1024,512]{1,0:T(8,128)(2,1)}, u32[]{:S(2)}) copy-start(bf16[1024,512]{1,0:T(8,128)(2,1)} %w2_hbm.1) | copy-start | bytes 3145732
  2.5 0.7 copy-start.2

commit v2 on v1

--- a/solution.py
+++ b/solution.py
@@ -27,7 +27,7 @@
     return ((0.5 * u) * (1.0 + jnp.tanh(inner))).astype(jnp.bfloat16)
 
 
-def kernel(x_hbm, g_hbm, w1_hbm, w2_hbm, y_hbm, xs, gs, w1s, w2s, zs, acc, ys, load_sem, out_sem, send_sem, recv_sem):
+def kernel(x_hbm, g_hbm, w1_hbm, w2_hbm, ys, xs, gs, w1s, w2s, zs, acc, load_sem, send_sem, recv_sem):
     n_chunks = xs.shape[1]
     n_w2 = w2_hbm.shape[0] // PC
     rows1 = w1_hbm.shape[0]
@@ -114,6 +114,9 @@
         send("w2d", s)
         for i in (2 * s, 2 * s + 1):
             loads[("x", i)].wait()
+            if i == n_chunks - 1:
+                for e in range(8):
+                    send("w1y", e)
             send("x", i)
 
     def layer_norm(i):
@@ -147,62 +150,80 @@
     def run(lo, hi, f):
         lax.fori_loop(lo, hi, lambda t, _: (f(t), 0)[1], 0)
 
-    issue(0)
-    issue(1)
-    arrive("g", 0)
+    def pair_tiles(chunks, half, j):
+        lo, hi = chunks
+        run(lo, hi, lambda c: tile(c, pair(half, j)))
+
+    def forward(j):
+        for e in (2 * j, 2 * j + 1):
+            arrive("w1y", e)
+            send("w1yx", e)
+            send("w1yd", e)
+
+    last = n_chunks - 1
+    with jax.named_scope("issue"):
+        issue(0)
+        issue(1)
+        arrive("g", 0)
     for s in range(4):
-        if s + 2 < 4:
-            issue(s + 2)
-        if s == 2:
-            for e in range(8):
-                send("w1y", e)
-        for e in (2 * s, 2 * s + 1):
-            arrive("w1x", e)
-            send("w1xd", e)
-        arrive("w2x", s)
-        send("w2xd", s)
-        for i in (2 * s, 2 * s + 1):
-            arrive("x", i)
-            layer_norm(i)
-        for e in (2 * s, 2 * s + 1):
-            arrive("w1d", e)
-            arrive("w1xd", e)
-        arrive("w2d", s)
-        arrive("w2xd", s)
-        run(0, 2 * s + 2, lambda c: tile(c, pair(col, s)))
-        if s > 0:
-            run(0, 2 * s, lambda t: tile(2 * s + t % 2, pair(col, t // 2)))
-
-    def forward(e):
-        arrive("w1y", e)
-        send("w1yx", e)
-        send("w1yd", e)
-
-    forward(0)
-    forward(1)
-    for e in range(8):
-        if e + 2 < 8:
-            forward(e + 2)
-        arrive("w1yx", e)
-        send("w1dd", e)
-        arrive("w1yd", e)
-        arrive("w1dd", e)
-        p = piece(other, e)
-        if e < 7:
-            run(0, n_chunks, lambda c: tile(c, (p,)))
-        else:
-            def last(c):
-                tile(c, (p,))
-                ys[c] = acc[c].astype(jnp.bfloat16)
-                pltpu.make_async_copy(ys.at[c], y_hbm.at[c], out_sem.at[c]).start()
-
-            run(0, n_chunks, last)
-
-    for kind, count in KINDS.items():
-        for i in range(count):
-            copy(kind, i, table[kind][1](i)).wait_send()
-    for c in range(n_chunks):
-        pltpu.make_async_copy(ys.at[c], y_hbm.at[c], out_sem.at[c]).wait()
+        with jax.named_scope(f"a_wait_x{s}"):
+            if s + 2 < 4:
+                issue(s + 2)
+            for e in (2 * s, 2 * s + 1):
+                arrive("w1x", e)
+                send("w1xd", e)
+            arrive("w2x", s)
+            send("w2xd", s)
+        new = range(2 * s, min(2 * s + 2, last))
+        with jax.named_scope(f"a_wait_y{s}"):
+            for i in new:
+                arrive("x", i)
+        with jax.named_scope(f"a_norm{s}"):
+            for i in new:
+                layer_norm(i)
+        with jax.named_scope(f"a_wait_d{s}"):
+            for e in (2 * s, 2 * s + 1):
+                arrive("w1d", e)
+                arrive("w1xd", e)
+            arrive("w2d", s)
+            arrive("w2xd", s)
+        with jax.named_scope(f"a_tiles{s}"):
+            pair_tiles((0, new[-1] + 1), col, s)
+            if s > 0:
+                run(0, s * len(new), lambda t: tile(2 * s + t % len(new), pair(col, t // len(new))))
+
+    with jax.named_scope("b_wait_first"):
+        forward(0)
+    for j in range(4):
+        with jax.named_scope(f"b_wait_y{j}"):
+            if j < 3:
+                forward(j + 1)
+        with jax.named_scope(f"b_wait_x{j}"):
+            for e in (2 * j, 2 * j + 1):
+                arrive("w1yx", e)
+                send("w1dd", e)
+        with jax.named_scope(f"b_wait_d{j}"):
+            for e in (2 * j, 2 * j + 1):
+                arrive("w1yd", e)
+                arrive("w1dd", e)
+        with jax.named_scope(f"b_tiles{j}"):
+            pair_tiles((0, last), other, j)
+
+    with jax.named_scope("c_wait"):
+        arrive("x", last)
+    with jax.named_scope("c_norm"):
+        layer_norm(last)
+    with jax.named_scope("c_tiles"):
+        run(0, 8, lambda t: tile(last, pair(t // 4, t % 4)))
+
+    with jax.named_scope("out"):
+        def write(c):
+            ys[c] = acc[c].astype(jnp.bfloat16)
+
+        run(0, n_chunks, write)
+        for kind, count in KINDS.items():
+            for i in range(count):
+                copy(kind, i, table[kind][1](i)).wait_send()
 
 
 def solution(mesh):
@@ -219,8 +240,8 @@
             kernel,
             name="mlp",
             out_shape=jax.ShapeDtypeStruct((n_chunks, TC, feats), jnp.bfloat16),
-            in_specs=[pl.BlockSpec(memory_space=pl.ANY)] * 4,
-            out_specs=pl.BlockSpec(memory_space=pl.ANY),
+            in_specs=[pl.BlockSpec(memory_space=pltpu.HBM)] * 4,
+            out_specs=pl.BlockSpec(memory_space=pltpu.VMEM),
             scratch_shapes=[
                 pltpu.VMEM((2, n_chunks, TC, feats), jnp.bfloat16),
                 pltpu.VMEM((2, 1, feats), jnp.float32),
@@ -228,14 +249,12 @@
                 pltpu.VMEM((n_pieces, PC, feats), jnp.bfloat16),
                 pltpu.VMEM((n_chunks, TC, d_model), jnp.bfloat16),
                 pltpu.VMEM((n_chunks, TC, feats), jnp.float32),
-                pltpu.VMEM((n_chunks, TC, feats), jnp.bfloat16),
                 pltpu.SemaphoreType.DMA((n_loads,)),
-                pltpu.SemaphoreType.DMA((n_chunks,)),
                 pltpu.SemaphoreType.DMA((N_COPIES,)),
                 pltpu.SemaphoreType.DMA((N_COPIES,)),
             ],
-            compiler_params=pltpu.CompilerParams(collective_id=0, has_side_effects=True, vmem_limit_bytes=48 * 1024 * 1024),
-        )(x_blk.reshape(n_chunks, TC, feats), gamma_blk.reshape(1, feats), w_in_blk, w_out_blk)
+            compiler_params=pltpu.CompilerParams(collective_id=0, has_side_effects=True, vmem_limit_bytes=52000000),
+        )(*[pltpu.with_memory_space_constraint(a, pltpu.HBM) for a in (x_blk.reshape(n_chunks, TC, feats), gamma_blk.reshape(1, feats), w_in_blk, w_out_blk)])
         return y.reshape(x_blk.shape)
 
     return jax.shard_map(per_device, mesh=mesh, in_specs=(act_spec, P("col"), P("row", "col"), P("row", "col")), out_specs=act_spec, check_vma=False)

time: 120 us -> 103 us (0.86)
  Pallas kernels: 116 us -> 101 us
  local copies, waits for them, and re-layouts: 4.45 us -> 1.32 us
    pallas_call x1, Pallas kernels: 116 us -> 101 us  [per_device(): pl.pallas_call(kernel, name='mlp', out_shape=jax.ShapeDtypeStruct((n_chun...]
    unnamed x7 -> x1, local copies, waits for them, and re-layouts: 4.45 us -> 1.32 us
where the time goes in v2:
time: 103 us
  Pallas kernels  101 us (98%)
  local copies, waits for them, and re-layouts  1.32 us (1%)
    pallas_call x1, Pallas kernels, per_device(): pl.pallas_call(kernel, name='mlp', out_shape=jax.ShapeDtypeStruct((n_chun...  101 us

profile of v2, /device:TPU:0, one launch (start us, length us, event | category | flops | bytes accessed | tf_op | source)
XLA Modules:
  0.0 102.5 jit_solution(5635303707235204012)
XLA Ops:
  0.0 101.2 %mlp.1 = bf16[8,256,512]{2,1,0:T(8,128)(2,1)S(1)} custom-call(bf16[8,256,512]{2,1,0:T(8,128)(2,1)} %bitcast.4, f32[1,512]{1,0:T(1,128)} %bitcast.5, bf16[256,2048]{1,0:T(8,128)(2,1)} %w1_hbm.1, bf16[1024,512]{1,0:T(8,128)(2,1)} %w2_hbm.1), custom_call_target="tpu_custom_call" | custom-call | tf_op jit(solution)/shard_map/mlp/pallas_call | solution.py:239
  101.2 1.3 %copy.6 = bf16[2,1024,512]{2,1,0:T(8,128)(2,1)} copy(bf16[2,1024,512]{2,1,0:T(8,128)(2,1)S(1)} %bitcast.3) | data formatting | bytes 4194304
